TPU v7x, 1024 devices: a whole 8x8x8 slice. The times are simulated.
1024 devices in a mesh: grp: 64 (over x, z), ep: 16 (over y, core).
Axes of the slice: x: 8, y: 8, z: 8, core: 2. Of those that a mesh axis runs over, the one named last changes fastest.
Arguments:
- out_grad: bfloat16 [8192, 4096], P('grp', 'ep'), may hold values from -6 to 6
- expert_ids: int32 [8192, 8], P('grp'), may hold values from 0 to 127, as said below
- router_logits: float32 [8192, 128], P('grp'), may hold values from -5 to 5
- router_weight: bfloat16 [128, 4096], P(None, 'ep'), may hold values from -0.09375 to 0.09375
- expert_weight: bfloat16 [128, 4096, 1024], P('grp', 'ep'), may hold values from -0.1875 to 0.1875
- hidden_saved: bfloat16 [64, 2048, 1024], P('grp'), may hold values from -6 to 6
Outputs:
- weight_grad: bfloat16 [128, 4096, 1024], P('grp', 'ep')
- hidden_grad: bfloat16 [64, 2048, 1024], P('grp', 'ep')
- input_grad: bfloat16 [8192, 4096], P('grp', 'ep')
Inputs may be any that keep to these rules, and one draw needn't show every extreme that they name: `expert_ids`: each row names 8 different experts, lying in at most 4 of the 8 groups of 16 consecutive experts. In each aligned block of 128 rows no expert is named by more than 16 rows, and some expert is named by exactly 16.
All inputs are finite; a program needn't handle non-finite values.
Results may differ from a plain program's by a relative error of at most 0.02.
Values may be sent and summed in bfloat16 or wider, within the bound.
A program may use at most 64 MiB of HBM per device.

v0:
```python
import jax
import jax.numpy as jnp
from jax import lax
from jax.sharding import PartitionSpec as P

route_scale = 2.5


def from_everyone(x, axis):
    count = lax.axis_size(axis)
    return lax.all_to_all(jnp.broadcast_to(x[None], (count, *x.shape)), axis, 0, 0, tiled=True)


def of_everyone(x, axis):
    return from_everyone(x, axis).sum(axis=0)


def body(out_grad, expert_ids, router_logits, router_weight, expert_weight, hidden_saved):
    group_rows, features = out_grad.shape
    top_count = expert_ids.shape[1]
    experts = router_logits.shape[1]
    group_count = lax.axis_size("grp")
    local_experts = expert_weight.shape[0]
    hidden_width = expert_weight.shape[2]
    slot_count = hidden_saved.shape[1]
    capacity = slot_count // (local_experts * group_count)
    expert_span = group_count * capacity
    pair_count = group_rows * top_count
    sig_values = jax.nn.sigmoid(router_logits)
    picked = expert_ids[:, :, None] == jnp.arange(experts, dtype=jnp.int32)[None, None, :]
    chosen = jnp.sum(jnp.where(picked, sig_values[:, None, :], 0.0), axis=2)
    route_probs = route_scale * chosen / jnp.sum(chosen, axis=1, keepdims=True)
    flat_ids = expert_ids.reshape(pair_count)
    onehot = picked.reshape(pair_count, experts).astype(jnp.int32)
    pair_ranks = jnp.sum((jnp.cumsum(onehot, axis=0) - 1) * onehot, axis=1)
    slot_place = (
        flat_ids % local_experts * group_count + flat_ids // local_experts
    ) * capacity + pair_ranks
    slot_match = slot_place[None, :] == jnp.arange(slot_count, dtype=jnp.int32)[:, None]
    token_pick = jnp.sum(
        slot_match.reshape(slot_count, group_rows, top_count).astype(jnp.float32), axis=2
    ).astype(jnp.bfloat16)
    send_rows = jnp.dot(token_pick, out_grad, preferred_element_type=jnp.float32).astype(
        jnp.bfloat16
    )
    send_prob = jnp.sum(
        jnp.where(slot_match, route_probs.reshape(1, pair_count), 0.0), axis=1
    ).astype(jnp.bfloat16)
    got_rows, got_prob = (
        lax.all_to_all(
            send_rows.reshape(local_experts, group_count, capacity, features),
            "grp",
            split_axis=1,
            concat_axis=1,
            tiled=True,
        ),
        lax.all_to_all(
            send_prob.reshape(local_experts, group_count, capacity),
            "grp",
            split_axis=1,
            concat_axis=1,
            tiled=True,
        ),
    )
    slot_grads = got_rows.reshape(local_experts, expert_span, features)
    prob_rows = got_prob.reshape(local_experts, expert_span).astype(jnp.float32)
    saved_rows = hidden_saved.reshape(local_experts, expert_span, hidden_width)
    scaled_rows = (prob_rows[:, :, None] * slot_grads.astype(jnp.float32)).astype(jnp.bfloat16)
    weight_grad = jnp.einsum(
        "lmd,lmf->ldf", scaled_rows, saved_rows, preferred_element_type=jnp.float32
    ).astype(jnp.bfloat16)
    owner_index = lax.axis_index("ep")
    share_rows = slot_count // lax.axis_size("ep")
    flat_prob = prob_rows.reshape(slot_count)
    flat_saved = hidden_saved.reshape(slot_count, hidden_width)
    partial_term = jnp.einsum(
        "lmd,ldf->lmf", slot_grads, expert_weight, preferred_element_type=jnp.float32
    ).reshape(slot_count, hidden_width)
    rounded_term = lax.optimization_barrier(partial_term.astype(jnp.bfloat16)).astype(jnp.float32)
    partial_score = jnp.sum(flat_saved.astype(jnp.float32) * rounded_term, axis=1)
    moved_scores = lax.all_to_all(
        partial_score.reshape(local_experts, group_count, capacity),
        "grp",
        split_axis=1,
        concat_axis=1,
        tiled=True,
    )
    returned = of_everyone(moved_scores, "ep")
    summed = lax.psum_scatter(
        partial_term.astype(jnp.bfloat16), "ep", scatter_dimension=0, tiled=True
    ).astype(jnp.float32)
    own_prob = lax.dynamic_slice_in_dim(flat_prob, owner_index * share_rows, share_rows, 0)
    hidden_grad = (own_prob[:, None] * summed).astype(jnp.bfloat16)[None]
    pair_score = jnp.sum(
        jnp.where(slot_match, returned.reshape(slot_count, 1), 0.0), axis=0
    ).reshape(group_rows, top_count)
    weighted_mean = jnp.sum(route_probs * pair_score, axis=1, keepdims=True) / route_scale
    logit_terms = route_probs * (1.0 - chosen) * (pair_score - weighted_mean)
    router_grad = jnp.sum(jnp.where(picked, logit_terms[:, :, None], 0.0), axis=1).astype(
        jnp.bfloat16
    )
    input_grad = jnp.dot(router_grad, router_weight, preferred_element_type=jnp.float32).astype(
        jnp.bfloat16
    )
    return (weight_grad, hidden_grad, input_grad)


def solution(mesh):
    in_specs = (
        P("grp", "ep"),
        P("grp", None),
        P("grp", None),
        P(None, "ep"),
        P("grp", "ep", None),
        P("grp", None, None),
    )
    out_specs = (P("grp", "ep", None), P("grp", "ep", None), P("grp", "ep"))
    return jax.shard_map(body, mesh=mesh, in_specs=in_specs, out_specs=out_specs, check_vma=False)
```

profile of v0, /device:TPU:1, one launch (start us, length us, event | category | flops | bytes accessed | tf_op | source)
XLA Modules:
  0.0 154.6 jit_solution(9558834379683258122)
XLA Ops:
  7.2 0.9 copy.76
  8.1 0.1 reshape.193
  8.2 0.1 eq.55
  8.3 0.1 copy.78
  8.4 0.2 fusion.4
  8.7 0.1 copy.79
  8.8 0.4 fusion.2
  9.2 0.1 reduce_sum.96
  9.3 0.7 fusion.16
  10.0 10.7 %convert_reduce_fusion = bf16[2048,128]{1,0:T(8,128)(2,1)S(1)} fusion(s32[128,8]{0,1:T(8,128)S(1)} %fusion.16), kind=kLoop, calls=%fused_computation.3 | loop fusion | flops 6029312 | bytes 528384 | tf_op jit(solution)/shard_map/reduce_sum | solution.py:40
  20.8 0.4 convolution_convert_fusion.1
  21.2 0.1 copy.85
  21.3 49.8 %all_to_all.20 = bf16[2,64,16,256]{3,2,0,1:T(8,128)(2,1)S(1)} all-to-all(bf16[2,64,16,256]{3,2,0,1:T(8,128)(2,1)S(1)} %copy.85), channel_id=1, replica_groups=mesh['grp'=64,'ep'=16] {'grp'}, dimensions={1} | all-to-all | bytes 2097152 | tf_op jit(solution)/shard_map/all_to_all | solution.py:50
  71.1 0.1 copy.86
  71.2 3.2 %convolution_convert_fusion = bf16[2,1024,1024]{2,1,0:T(8,128)(2,1)} fusion(bf16[2,1024,256]{2,1,0:T(8,128)(2,1)S(1)} %bitcast.32, bf16[2,256,1024]{2,1,0:T(8,128)(2,1)S(1)} %copy-done), kind=kOutput, calls=%fused_computation.7 | convolution fusion | flops 1075838976 | bytes 6291456 | tf_op jit(solution)/shard_map/lmd,ldf->lmf/dot_general | solution.py:76
  74.5 4.6 %fusion = f32[2048]{0:T(1024)S(1)} fusion(bf16[2048,1024]{1,0:T(8,128)(2,1)} %bitcast.29, bf16[1,2048,1024]{2,1,0:T(8,128)(2,1)} %param.11), kind=kLoop, calls=%fused_computation.1 | loop fusion | flops 8386560 | bytes 8396800 | tf_op jit(solution)/shard_map/reduce_sum | solution.py:80
  79.1 0.1 reshape.198
  79.2 0.7 copy.89
  79.9 8.9 %all-to-all-start.2 = ((f32[2,64,16]{2,0,1:T(2,128)}), f32[2,64,16]{2,0,1:T(2,128)S(1)}, u32[]{:S(2)}, u32[]{:S(2)}) async-start(f32[2,64,16]{2,0,1:T(2,128)} %copy.89), calls=%async_computation.3 | async-start | bytes 131072 | tf_op jit(solution)/shard_map/all_to_all | solution.py:81
  88.8 2.0 %select_reduce_fusion.2 = (f32[128]{0:T(128)S(1)}, f32[128,8]{1,0:T(8,128)S(1)}) fusion(f32[128,128]{1,0:T(8,128)S(1)} %add_divide_fusion, s32[128,8]{1,0:T(8,128)S(1)} %copy.76), kind=kLoop, calls=%fused_computation.13 | loop fusion | flops 523136 | bytes 74240 | tf_op jit(solution)/shard_map/reduce_sum | solution.py:32
  90.8 9.1 %all-to-all-done.2 = f32[2,64,16]{2,0,1:T(2,128)S(1)} async-done(((f32[2,64,16]{2,0,1:T(2,128)}), f32[2,64,16]{2,0,1:T(2,128)S(1)}, u32[]{:S(2)}, u32[]{:S(2)}) %all-to-all-start.2) | async-done | bytes 8224 | tf_op jit(solution)/shard_map/all_to_all | solution.py:81
  100.0 0.8 reshape.203
  100.8 10.0 %all-to-all-start.3 = ((f32[16,1,2048]{2,1,0:T(1,128)}), f32[16,1,2048]{2,1,0:T(1,128)S(1)}, u32[]{:S(2)}, u32[]{:S(2)}) async-start(f32[16,1,2048]{2,1,0:T(1,128)} %reshape.203), calls=%async_computation.4 | async-start | bytes 262144 | tf_op jit(solution)/shard_map/all_to_all | solution.py:11
  110.9 0.1 multiply_divide_fusion
  111.0 0.1 div.50
  111.1 9.6 %all-to-all-done.3 = f32[16,1,2048]{2,1,0:T(1,128)S(1)} async-done(((f32[16,1,2048]{2,1,0:T(1,128)}), f32[16,1,2048]{2,1,0:T(1,128)S(1)}, u32[]{:S(2)}, u32[]{:S(2)}) %all-to-all-start.3) | async-done | bytes 131104 | tf_op jit(solution)/shard_map/all_to_all | solution.py:11
  120.7 0.5 broadcast.174
  121.2 1.0 reduce.1
  122.2 0.1 reshape.204
  122.3 0.1 copy.91
  122.4 0.1 broadcast_in_dim.71
  122.5 2.4 %select_reduce_fusion = (f32[1024]{0:T(1024)S(1)}, bf16[2048]{0:T(1024)(128)(2,1)S(1)}) fusion(f32[2048]{0:T(1024)S(1)} %broadcast_in_dim.71, s32[1024]{0:T(1024)S(1)} %fusion.12, f32[1024]{0:T(1024)S(1)} %div.50), kind=kLoop, calls=%fused_computation.2 | loop fusion | flops 10482688 | bytes 24576 | tf_op jit(solution)/shard_map/reduce_sum | solution.py:94
  124.8 0.1 convert_element_type.76
  124.9 0.7 copy.81
  125.6 4.6 %all-to-all-start = ((bf16[2,64,16]{2,0,1:T(2,128)(2,1)}), bf16[2,64,16]{2,0,1:T(2,128)(2,1)S(1)}, u32[]{:S(2)}, u32[]{:S(2)}) async-start(bf16[2,64,16]{2,0,1:T(2,128)(2,1)} %copy.81), calls=%async_computation | async-start | bytes 65536 | tf_op jit(solution)/shard_map/all_to_all | solution.py:57
  130.2 0.1 reshape.199
  130.3 0.2 multiply_reduce_fusion
  130.5 0.1 subtract_multiply_fusion
  130.6 0.4 select_reduce_fusion.4
  131.0 0.8 convolution_convert_fusion.3
  131.7 9.2 %all-to-all-done = bf16[2,64,16]{2,0,1:T(2,128)(2,1)S(1)} async-done(((bf16[2,64,16]{2,0,1:T(2,128)(2,1)}), bf16[2,64,16]{2,0,1:T(2,128)(2,1)S(1)}, u32[]{:S(2)}, u32[]{:S(2)}) %all-to-all-start) | async-done | bytes 4128 | tf_op jit(solution)/shard_map/all_to_all | solution.py:57
  141.0 0.1 copy.82
  141.0 0.1 copy.83
  141.1 0.1 reshape.201
  141.2 0.1 reshape.200
  141.3 0.1 dynamic_slice.3
  141.4 4.6 %convolution_convert_fusion.2 = bf16[2,256,1024]{2,1,0:T(8,128)(2,1)} fusion(bf16[2,1024,1024]{2,1,0:T(8,128)(2,1)} %bitcast.30, bf16[2,1024,256]{2,1,0:T(8,128)(2,1)S(1)} %bitcast.33, f32[2,1024]{1,0:T(2,128)S(1)} %reshape.200), kind=kOutput, calls=%fused_computation.10 | convolution fusion | flops 1075838976 | bytes 6299648 | tf_op jit(solution)/shard_map/lmd,lmf->ldf/dot_general | solution.py:69
  146.0 1.8 %fusion.6 = bf16[1,128,1024]{2,1,0:T(8,128)(2,1)} fusion(bf16[128,1024]{1,0:T(8,128)(2,1)} %reduce-scatter.2.cloned.1.call-done, f32[128]{0:T(128)S(1)} %dynamic_slice.3), kind=kLoop, calls=%fused_computation.26 | loop fusion | flops 393216 | bytes 524800 | tf_op jit(solution)/shard_map/broadcast_in_dim | solution.py:93
  (22 shorter events, 0.4 us)
Async XLA Ops:
  7.2 64.0 %copy-start = (bf16[2,256,1024]{2,1,0:T(8,128)(2,1)S(1)}, bf16[2,256,1024]{2,1,0:T(8,128)(2,1)}, u32[]{:S(2)}) copy-start(bf16[2,256,1024]{2,1,0:T(8,128)(2,1)} %param.10) | copy-start | bytes 3145732
  7.2 13.6 %copy-start.1 = (bf16[128,256]{1,0:T(8,128)(2,1)S(1)}, bf16[128,256]{1,0:T(8,128)(2,1)}, u32[]{:S(2)}) copy-start(bf16[128,256]{1,0:T(8,128)(2,1)} %param.6) | copy-start | bytes 196612
  7.2 138.8 %reduce-scatter.2.cloned.1.call-start = ((), (), s32[]{:S(2)}) async-start(), calls=%async_computation.5 | async-start | bytes 4456448 | tf_op jit(solution)/shard_map/reduce_scatter | solution.py:89
  71.2 3.2 %copy-start.2 = (f32[128,128]{1,0:T(8,128)S(1)}, f32[128,128]{1,0:T(8,128)}, u32[]{:S(2)}) copy-start(f32[128,128]{1,0:T(8,128)} %param.8) | copy-start | bytes 196612
  74.5 56.5 %copy-start.3 = (bf16[128,256]{1,0:T(8,128)(2,1)S(1)}, bf16[128,256]{1,0:T(8,128)(2,1)}, u32[]{:S(2)}) copy-start(bf16[128,256]{1,0:T(8,128)(2,1)} %param.9) | copy-start | bytes 196612
  79.9 20.0 %all-to-all-start.2 = ((f32[2,64,16]{2,0,1:T(2,128)}), f32[2,64,16]{2,0,1:T(2,128)S(1)}, u32[]{:S(2)}, u32[]{:S(2)}) async-start(f32[2,64,16]{2,0,1:T(2,128)} %copy.89), calls=%async_computation.3 | async-start | bytes 131072 | tf_op jit(solution)/shard_map/all_to_all | solution.py:81
  100.8 19.8 %all-to-all-start.3 = ((f32[16,1,2048]{2,1,0:T(1,128)}), f32[16,1,2048]{2,1,0:T(1,128)S(1)}, u32[]{:S(2)}, u32[]{:S(2)}) async-start(f32[16,1,2048]{2,1,0:T(1,128)} %reshape.203), calls=%async_computation.4 | async-start | bytes 262144 | tf_op jit(solution)/shard_map/all_to_all | solution.py:11
  125.6 15.4 %all-to-all-start = ((bf16[2,64,16]{2,0,1:T(2,128)(2,1)}), bf16[2,64,16]{2,0,1:T(2,128)(2,1)S(1)}, u32[]{:S(2)}, u32[]{:S(2)}) async-start(bf16[2,64,16]{2,0,1:T(2,128)(2,1)} %copy.81), calls=%async_computation | async-start | bytes 65536 | tf_op jit(solution)/shard_map/all_to_all | solution.py:57
Sparse Core Ops, SparseCore 0:
  74.5 68.2 reduce-scatter.1
where the time goes:
time: 155 us
  blocking collectives  49.8 us (32%)
  waiting for transfers between devices  28 us (18%)
  other arithmetic  24.6 us (16%)
  starting transfers between devices  23.5 us (15%)
  between operations  14.3 us (9%)
  matrix products  8.97 us (6%)
  local copies, waits for them, and re-layouts  5.46 us (4%)
    all_to_all x1, blocking collectives, body(): lax.all_to_all(send_rows.reshape(local_experts, group_count, capacity, fe...  49.8 us
    reduce_sum x1, other arithmetic, body(): jnp.sum(slot_match.reshape(slot_count, group_rows, top_count).astype(jnp....  10.7 us
    all_to_all x1, starting transfers between devices, from_everyone(): lax.all_to_all(jnp.broadcast_to(x[None], (count, *x.shape)), axis, 0, 0,...  10 us
    all_to_all x1, waiting for transfers between devices, from_everyone(): lax.all_to_all(jnp.broadcast_to(x[None], (count, *x.shape)), axis, 0, 0,...  9.61 us
    all_to_all x1, waiting for transfers between devices, body(): lax.all_to_all(send_prob.reshape(local_experts, group_count, capacity), '...  9.22 us
    all_to_all x1, waiting for transfers between devices, body(): lax.all_to_all(partial_score.reshape(local_experts, group_count, capacity...  9.13 us
    all_to_all x1, starting transfers between devices, body(): lax.all_to_all(partial_score.reshape(local_experts, group_count, capacity...  8.86 us
    reduce_sum x1, other arithmetic, body(): jnp.sum(flat_saved.astype(jnp.float32) * rounded_term, axis=1)  4.65 us
  transfers between devices with their start and end apart: 4, of which 3 were waited for; matrix products, arithmetic and copies ran while one was open for 13% of the time, Pallas kernels for 0%

commit v1 on v0

v1 whole, which is shorter than its diff:
```python
import functools
import jax
import jax.numpy as jnp
from jax import lax
from jax.experimental import pallas as pl
from jax.experimental.pallas import tpu as pltpu
from jax.sharding import PartitionSpec as P

route_scale = 2.5
cap = 16
unset = 255.0
bf16 = jnp.bfloat16
f32 = jnp.float32
MESH = pl.DeviceIdType.MESH


def iota(shape, dim):
    return lax.broadcasted_iota(jnp.int32, shape, dim)


def kernel(n, og_ref, ids_ref, lg_ref, rw_ref, ew_ref, hs_ref, wg_ref, hg_ref, ig_ref,
           hs_v, w_v, wp_v, tok, tk, tbs0, tbs1, tb0, tb1, sb0, sb1, r0, r1, e0, e1,
           dacc, ds, dr, g_v, pb, sr, wg_v, s_v, sa, bs, sc, ct, q_s, q_c, q_y, q_r,
           acc, snd, rcv, code_v, prob_v, sig_v,
           loc_sem, s1_send, s1_recv, s2_send, s2_recv, d_send, d_recv, x_send, x_recv,
           a_send, a_recv, b_send, b_recv, y_send, y_recv, r_send, r_recv):
    tokens, half = og_ref.shape[0], og_ref.shape[1] // 2
    topk = ids_ref.shape[1]
    experts = lg_ref.shape[1]
    width = hs_v.shape[1]
    ge = 2 * n
    hn = n // 2
    ch = n * cap
    rows = hn * cap
    subs = min(2, hn)
    sub = rows // subs
    g = lax.axis_index("grp")
    k = lax.axis_index("ep")
    x, z = g // n, lax.rem(g, n)
    y, c = k // 2, lax.rem(k, 2)
    wrap = lambda v: lax.rem(v + 2 * n, n)
    at_x = lambda v: (v * n + z, k)
    at_z = lambda v: (x * n + v, k)
    at_y = lambda v: (g, v * 2 + c)
    partner = (g, y * 2 + 1 - c)

    def rcopy(src, dst, ss, rs, dev):
        return pltpu.make_async_remote_copy(
            src_ref=src, dst_ref=dst, send_sem=ss, recv_sem=rs, device_id=dev, device_id_type=MESH)

    w_in = pltpu.make_async_copy(ew_ref, w_v, loc_sem.at[0])
    w_in.start()
    hs_in = pltpu.make_async_copy(hs_ref, hs_v, loc_sem.at[1])
    hs_in.start()
    barrier = pltpu.get_barrier_semaphore()
    for d in range(1, n):
        for at, me in ((at_x, x), (at_z, z), (at_y, y)):
            pl.semaphore_signal(barrier, inc=1, device_id=at(wrap(me + d)), device_id_type=MESH)
    pl.semaphore_signal(barrier, inc=1, device_id=partner, device_id_type=MESH)

    ids = ids_ref[...]
    lane_e = iota((tokens, experts), 1)
    member = jnp.zeros((tokens, experts), f32)
    for i in range(topk):
        member += (ids[:, i:i + 1] == lane_e).astype(f32)
    lower = (iota((tokens, tokens), 0) > iota((tokens, tokens), 1)).astype(f32).astype(bf16)
    rank = jnp.dot(lower, member.astype(bf16), preferred_element_type=f32)
    code = jnp.where(member > 0.0, rank, unset)
    sig = jax.nn.sigmoid(lg_ref[...])
    chosen = member * sig
    prob = route_scale * chosen / jnp.sum(chosen, axis=1, keepdims=True)
    code_v[...] = code
    prob_v[...] = prob
    sig_v[...] = sig
    code_t = code.T
    prob_t = prob.T.astype(bf16)
    row_e, col_e = iota((experts, experts), 0), iota((experts, experts), 1)
    perm = (col_e == (row_e // 2 % n) * ge + (row_e // ge) * 2 + row_e % 2).astype(f32).astype(bf16)
    code_t = code_t.astype(bf16)
    code_p = jnp.dot(perm, code_t, preferred_element_type=f32).astype(bf16)
    for v in range(n):
        tbs0[v, 0:ge, :] = code_t[v * ge:(v + 1) * ge, :]
        tbs0[v, ge:2 * ge, :] = prob_t[v * ge:(v + 1) * ge, :]
        tbs1[v] = code_p[v * ge:(v + 1) * ge, :]
    og = og_ref[...]
    tok[0] = og[:, :half]
    tok[1] = og[:, half:]
    tk[0, x] = og[:, :half]
    tk[1, z] = og[:, half:]
    tb0[x] = tbs0[x]
    tb1[z] = tbs1[z]

    pl.semaphore_wait(barrier, 3 * (n - 1) + 1)

    order = [d if i == 0 else n - d for d in range(1, hn + 1) for i in range(2)][: n - 1]

    def tok0(v):
        return rcopy(tok.at[0], tk.at[0, x], s1_send.at[0, v], s1_recv.at[0, x], at_x(v))

    def tok1(v):
        return rcopy(tok.at[1], tk.at[1, z], s1_send.at[1, v], s1_recv.at[1, z], at_z(v))

    def tab0(v):
        return rcopy(tbs0.at[v], tb0.at[x], s1_send.at[2, v], s1_recv.at[2, x], at_x(v))

    def tab1(v):
        return rcopy(tbs1.at[v], tb1.at[z], s1_send.at[3, v], s1_recv.at[3, z], at_z(v))

    for d in order:
        tab0(wrap(x + d)).start()
        tok0(wrap(x + d)).start()
        tab1(wrap(z + d)).start()
        tok1(wrap(z + d)).start()

    w_in.wait()
    w_out = rcopy(w_v, wp_v, x_send.at[0], x_recv.at[0], partner)
    w_out.start()

    slot_r = iota((ge, cap, tokens), 1).astype(f32)
    dacc[...] = jnp.zeros_like(dacc)

    def fill(path, table):
        hot = (table.astype(f32)[:, None, :] == slot_r).astype(f32).astype(bf16)
        hot = hot.reshape(ge * cap, tokens)
        return hot

    def out0(v, us):
        return rcopy(sb0.at[v, us], r0.at[z, us // 2, lax.rem(us, 2)], s2_send.at[0, v], s2_recv.at[0, z], at_z(v))

    def out1(v, us):
        return rcopy(sb1.at[v, us], r1.at[x // 2, lax.rem(x, 2), us], s2_send.at[1, v], s2_recv.at[1, x], at_x(v))

    def spread0(us):
        hot = fill(0, tb0[us, 0:ge, :])
        got = jnp.dot(hot, tk[0, us], preferred_element_type=f32).astype(bf16)
        sb0[:, us] = got.reshape(n, 2, cap, half)
        for d in order:
            out0(wrap(z + d), us).start()
        r0[z, us // 2, lax.rem(us, 2)] = sb0[z, us]
        table = tb0[us, ge:2 * ge, :]
        wide = jnp.concatenate([table] * n, axis=0)
        wide = jnp.where(iota((experts, tokens), 0) // ge == us, wide.astype(f32), 0.0).astype(bf16)
        dacc[...] += lax.dot_general(hot, wide, (((1,), (1,)), ((), ())), preferred_element_type=f32)

    def spread1(us):
        hot = fill(1, tb1[us])
        got = jnp.dot(hot, tk[1, us], preferred_element_type=f32).astype(bf16)
        sb1[:, us] = got.reshape(n, 2, cap, half)
        for d in order:
            out1(wrap(x + d), us).start()
        r1[x // 2, lax.rem(x, 2), us] = sb1[x, us]

    spread0(x)
    spread1(z)

    def arrive(j, carry):
        off = (j + 1) // 2
        off = jnp.where(lax.rem(j, 2) == 1, off, n - off)
        ux, uz = wrap(x + off), wrap(z + off)
        rcopy(tbs0.at[0], tb0.at[ux], s1_send.at[2, 0], s1_recv.at[2, ux], partner).wait_recv()
        rcopy(tok.at[0], tk.at[0, ux], s1_send.at[0, 0], s1_recv.at[0, ux], partner).wait_recv()
        spread0(ux)
        rcopy(tbs1.at[0], tb1.at[uz], s1_send.at[3, 0], s1_recv.at[3, uz], partner).wait_recv()
        rcopy(tok.at[1], tk.at[1, uz], s1_send.at[1, 0], s1_recv.at[1, uz], partner).wait_recv()
        spread1(uz)
        return carry

    lax.fori_loop(1, n, arrive, 0)

    ds[...] = dacc[...].astype(bf16).reshape(n, 2 * cap, experts)
    dr[z] = ds[z]

    def dout(v):
        return rcopy(ds.at[v], dr.at[z], d_send.at[v], d_recv.at[z], at_z(v))

    for d in order:
        dout(wrap(z + d)).start()

    hs_in.wait()
    tile = ch * n // 4

    def gmul(i, carry):
        l = i // 4
        at = pl.multiple_of(i * tile, tile)
        g_v[pl.ds(at, tile), :] = lax.dot_general(
            hs_v[pl.ds(at, tile), :], w_v[l], (((1,), (1,)), ((), ())), preferred_element_type=f32)
        return carry

    lax.fori_loop(0, 8, gmul, 0)

    for d in order:
        vz, vx = wrap(z + d), wrap(x + d)
        rcopy(sb0.at[0], r0.at[vz], s2_send.at[0, 0], s2_recv.at[0, vz], partner).wait_recv()
        rcopy(sb1.at[0], r1.at[vx // 2, lax.rem(vx, 2)], s2_send.at[1, 0], s2_recv.at[1, vx], partner).wait_recv()

    ex0 = rcopy(r0.at[:, :, 1 - c], e0, x_send.at[1], x_recv.at[1], partner)
    ex1 = rcopy(r1.at[:, 1 - c], e1, x_send.at[2], x_recv.at[2], partner)
    ex0.start()
    ex1.start()

    eye = iota((ch, ch), 0) == iota((ch, ch), 1)
    for l in range(2):
        for xb in range(n):
            q = l * n * ch + xb * ch
            a0 = r0[:, xb // 2, xb % 2, l].reshape(ch, half).astype(f32)
            a1 = r1[xb // 2, xb % 2, :, l].reshape(ch, half).astype(f32)
            s = a0 * g_v[q:q + ch, :half] + a1 * g_v[q:q + ch, half:]
            s = jnp.sum(s, axis=1, keepdims=True)
            s_v[l * n + xb:l * n + xb + 1, :] = jnp.sum(jnp.where(eye, s, 0.0), axis=0, keepdims=True)

    w_out.wait_recv()
    ex0.wait_recv()
    ex1.wait_recv()

    def partial(chunk, d):
        l, xh = chunk // hn, lax.rem(chunk, hn)
        zs = pl.ds(d * hn, hn)
        own = jnp.concatenate(
            [r0[zs, xh, c, l].reshape(rows, half), r1[xh, c, zs, l].reshape(rows, half)], axis=1)
        other = jnp.concatenate(
            [e0[zs, xh, l].reshape(rows, half), e1[xh, zs, l].reshape(rows, half)], axis=1)
        step = width // 4
        for j in range(4):
            cols = slice(j * step, (j + 1) * step)
            acc[d, :, cols] = jnp.dot(own, w_v[l, :, cols], preferred_element_type=f32) + jnp.dot(
                other, wp_v[l, :, cols], preferred_element_type=f32)

    def hop(s, d, i):
        to = at_y(wrap(y + 1)) if d == 0 else at_y(wrap(y - 1 + n))
        return rcopy(snd.at[d, s, i], rcv.at[d, s, i], r_send.at[d, s, i], r_recv.at[d, s, i], to)

    def ring(s):
        for d in range(2):
            partial(wrap(y - 1 - s + n) if d == 0 else wrap(y + 1 + s), d)
        for i in range(subs):
            for d in range(2):
                val = acc[d, i * sub:(i + 1) * sub, :]
                if s > 0:
                    hop(s - 1, d, i).wait_recv()
                    val = val + rcv[d, s - 1, i].astype(f32)
                snd[d, s, i] = val.astype(bf16)
                hop(s, d, i).start()

    def aout(v):
        return rcopy(s_v, sa.at[z], a_send.at[v], a_recv.at[z], at_z(v))

    def bout(v):
        return rcopy(bs.at[v], sc.at[x], b_send.at[v], b_recv.at[x], at_x(v))

    def yout(v):
        return rcopy(q_y, q_r.at[y], y_send.at[v], y_recv.at[y], at_y(v))

    qx = rcopy(q_s, q_c, x_send.at[3], x_recv.at[3], partner)

    def score_a():
        sa[z] = s_v[...]
        for d in order:
            aout(wrap(z + d)).start()

    def score_b():
        for d in order:
            v = wrap(z + d)
            rcopy(s_v, sa.at[v], a_send.at[0], a_recv.at[v], partner).wait_recv()
        for v in range(n):
            for l in range(2):
                for xb in range(n):
                    bs[xb, v * 2 + l:v * 2 + l + 1, :] = sa[v, l * n + xb:l * n + xb + 1, :]
        sc[x] = bs[x]
        for d in order:
            bout(wrap(x + d)).start()

    def score_c():
        for d in order:
            v = wrap(x + d)
            rcopy(bs.at[0], sc.at[v], b_send.at[0], b_recv.at[v], partner).wait_recv()
        ct[...] = sc[...].reshape(experts, ch).T
        q_s[...] = ct[pl.ds(pl.multiple_of(z * cap, cap), cap), :]
        qx.start()

    def score_d():
        qx.wait_recv()
        q_y[...] = q_s[...] + q_c[...]
        q_r[y] = q_y[...]
        for d in order:
            yout(wrap(y + d)).start()

    def finish():
        for d in order:
            v = wrap(y + d)
            rcopy(q_y, q_r.at[v], y_send.at[0], y_recv.at[v], partner).wait_recv()
        total = q_r[0]
        for v in range(1, n):
            total = total + q_r[v]
        codes = code_v[...]
        pair = jnp.zeros((tokens, experts), f32)
        for r in range(cap):
            pair += jnp.where(codes == float(r), total[r:r + 1, :], 0.0)
        probs = prob_v[...]
        mean = jnp.sum(probs * pair, axis=1, keepdims=True) / route_scale
        grad = (probs * (1.0 - sig_v[...]) * (pair - mean)).astype(bf16)
        ig_ref[...] = jnp.dot(grad, rw_ref[...], preferred_element_type=f32).astype(bf16)

    def probs_in():
        for d in order:
            v = wrap(z + d)
            rcopy(ds.at[0], dr.at[v], d_send.at[0], d_recv.at[v], partner).wait_recv()
        mine = dr[...].reshape(n * 2 * cap, experts).astype(f32)
        shape = (n * 2 * cap, experts)
        keep = iota(shape, 1) % ge == z * 2 + iota(shape, 0) // cap % 2
        mine = jnp.where(keep, mine, 0.0).astype(bf16)
        wide = (experts, n * half)
        pick = (iota(wide, 0) // ge == iota(wide, 1) // half).astype(f32).astype(bf16)
        pb[...] = jnp.dot(mine, pick, preferred_element_type=f32).reshape(n, 2, cap, n * half)
        for l in range(2):
            for xb in range(n):
                p = pb[:, l, :, xb * half:(xb + 1) * half].reshape(ch, half)
                a0 = r0[:, xb // 2, xb % 2, l].reshape(ch, half).astype(f32)
                a1 = r1[xb // 2, xb % 2, :, l].reshape(ch, half).astype(f32)
                sr[l, xb * ch:(xb + 1) * ch, :half] = (p * a0).astype(bf16)
                sr[l, xb * ch:(xb + 1) * ch, half:] = (p * a1).astype(bf16)

    wg_out = [pltpu.make_async_copy(wg_v.at[l], wg_ref.at[l], loc_sem.at[2 + l]) for l in range(2)]

    def grads(l):
        step = width // 4
        for j in range(4):
            cols = slice(j * step, (j + 1) * step)
            wg_v[l, :, cols] = lax.dot_general(
                sr[l], hs_v[l * n * ch:(l + 1) * n * ch, cols], (((0,), (0,)), ((), ())),
                preferred_element_type=f32).astype(bf16)
        wg_out[l].start()

    extra = {0: score_a, 1: score_b, 2: score_c, 3: score_d, 4: probs_in,
             5: lambda: grads(0), 6: lambda: grads(1)}
    if n < 8:
        todo = list(extra.values())
        extra = {0: lambda: [f() for f in todo]}
    for s in range(n - 1):
        ring(s)
        if s in extra:
            extra[s]()
    for d in range(2):
        partial(y, d)
    mine_l, mine_x = k // n, lax.rem(k, n)
    for i in range(subs):
        for d in range(2):
            hop(n - 2, d, i).wait_recv()
            val = acc[d, i * sub:(i + 1) * sub, :] + rcv[d, n - 2, i].astype(f32)
            zs = pl.ds(d * hn + i * (hn // subs), hn // subs)
            p = pb[zs, mine_l, :, pl.ds(pl.multiple_of(mine_x * half, half), half)].reshape(sub, half)
            for j in range(width // half):
                cols = slice(j * half, (j + 1) * half)
                at = d * rows + i * sub
                hg_ref[at:at + sub, cols] = (p * val[:, cols]).astype(bf16)
    finish()

    w_out.wait_send()
    ex0.wait_send()
    ex1.wait_send()
    qx.wait_send()
    for d in order:
        vx, vz, vy = wrap(x + d), wrap(z + d), wrap(y + d)
        tok0(vx).wait_send()
        tok1(vz).wait_send()
        tab0(vx).wait_send()
        tab1(vz).wait_send()
        rcopy(sb0.at[vz], r0.at[z], s2_send.at[0, vz], s2_recv.at[0, z], partner).wait_send()
        rcopy(sb1.at[vx], r1.at[x // 2, lax.rem(x, 2)], s2_send.at[1, vx], s2_recv.at[1, x], partner).wait_send()
        dout(vz).wait_send()
        aout(vz).wait_send()
        bout(vx).wait_send()
        yout(vy).wait_send()
    for s in range(n - 1):
        for i in range(subs):
            for d in range(2):
                hop(s, d, i).wait_send()
    for l in range(2):
        wg_out[l].wait()


def body(n, out_grad, expert_ids, router_logits, router_weight, expert_weight, hidden_saved):
    tokens, features = out_grad.shape
    half = features // 2
    experts = router_logits.shape[1]
    width = expert_weight.shape[2]
    slots = hidden_saved.shape[1]
    ge, hn, ch = 2 * n, n // 2, n * cap
    rows, subs = hn * cap, min(2, hn)
    vm = pltpu.VMEM
    dma = pltpu.SemaphoreType.DMA
    scratch = [
        vm((slots, width), bf16), vm((2, features, width), bf16), vm((2, features, width), bf16),
        vm((2, tokens, half), bf16), vm((2, n, tokens, half), bf16),
        vm((n, 2 * ge, tokens), bf16), vm((n, ge, tokens), bf16),
        vm((n, 2 * ge, tokens), bf16), vm((n, ge, tokens), bf16),
        vm((n, n, 2, cap, half), bf16), vm((n, n, 2, cap, half), bf16),
        vm((n, hn, 2, 2, cap, half), bf16), vm((hn, 2, n, 2, cap, half), bf16),
        vm((n, hn, 2, cap, half), bf16), vm((hn, n, 2, cap, half), bf16),
        vm((ge * cap, experts), f32), vm((n, 2 * cap, experts), bf16), vm((n, 2 * cap, experts), bf16),
        vm((slots, features), f32), vm((n, 2, cap, n * half), f32), vm((2, n * ch, features), bf16),
        vm((2, features, width), bf16),
        vm((ge, ch), f32), vm((n, ge, ch), f32), vm((n, ge, ch), f32), vm((n, ge, ch), f32),
        vm((ch, experts), f32),
        vm((cap, experts), f32), vm((cap, experts), f32), vm((cap, experts), f32), vm((n, cap, experts), f32),
        vm((2, rows, width), f32), vm((2, n - 1, subs, rows // subs, width), bf16),
        vm((2, n - 1, subs, rows // subs, width), bf16),
        vm((tokens, experts), f32), vm((tokens, experts), f32), vm((tokens, experts), f32),
        dma((4,)), dma((4, n)), dma((4, n)), dma((2, n)), dma((2, n)), dma((n,)), dma((n,)),
        dma((4,)), dma((4,)), dma((n,)), dma((n,)), dma((n,)), dma((n,)), dma((n,)), dma((n,)),
        dma((2, n - 1, subs)), dma((2, n - 1, subs)),
    ]
    in_vmem = pl.BlockSpec(memory_space=pltpu.VMEM)
    in_hbm = pl.BlockSpec(memory_space=pltpu.HBM)
    weight_grad, hidden_grad, input_grad = pl.pallas_call(
        functools.partial(kernel, n),
        out_shape=(
            jax.ShapeDtypeStruct((2, features, width), bf16),
            jax.ShapeDtypeStruct((ch, width), bf16),
            jax.ShapeDtypeStruct((tokens, features), bf16),
        ),
        in_specs=[in_vmem, in_vmem, in_vmem, in_vmem, in_hbm, in_hbm],
        out_specs=(in_hbm, in_vmem, in_vmem),
        scratch_shapes=scratch,
        compiler_params=pltpu.CompilerParams(collective_id=0, has_side_effects=True),
    )(out_grad, expert_ids, router_logits, router_weight, expert_weight, hidden_saved.reshape(slots, width))
    return weight_grad, hidden_grad[None], input_grad


def solution(mesh):
    n = mesh.shape["ep"] // 2
    in_specs = (
        P("grp", "ep"),
        P("grp", None),
        P("grp", None),
        P(None, "ep"),
        P("grp", "ep", None),
        P("grp", None, None),
    )
    out_specs = (P("grp", "ep", None), P("grp", "ep", None), P("grp", "ep"))
    return jax.shard_map(functools.partial(body, n), mesh=mesh, in_specs=in_specs, out_specs=out_specs, check_vma=False)
```

time: 155 us -> 84.7 us (0.55)
  Pallas kernels: 0 us -> 76 us
  blocking collectives: 49.8 us -> 0 us
  waiting for transfers between devices: 28 us -> 0 us
  other arithmetic: 24.6 us -> 0 us
  starting transfers between devices: 23.5 us -> 0 us
  between operations: 14.3 us -> 0.64 us
  matrix products: 8.97 us -> 0 us
    pallas_call x0 -> x1, Pallas kernels: none -> 76 us  [body(): pl.pallas_call(functools.partial(kernel, n), out_shape=(jax.ShapeDtypeStr...]
    all_to_all x1 -> x0, blocking collectives: 49.8 us -> none  [body(): lax.all_to_all(send_rows.reshape(local_experts, group_count, capacity, fe...]
    all_to_all x3 -> x0, waiting for transfers between devices: 28 us -> none  [the longest x1 9.61 us: from_everyone(): lax.all_to_all(jnp.broadcast_to(x[None], (count, *x.shape)), axis, 0, 0,...]
    all_to_all x3 -> x0, starting transfers between devices: 23.5 us -> none  [the longest x1 10 us: from_everyone(): lax.all_to_all(jnp.broadcast_to(x[None], (count, *x.shape)), axis, 0, 0,...]
    reduce_sum x8 -> x0, other arithmetic: 20.7 us -> none  [the longest x1 10.7 us: body(): jnp.sum(slot_match.reshape(slot_count, group_rows, top_count).astype(jnp....]
    dot_general x4 -> x0, matrix products: 8.97 us -> none  [the longest x1 4.59 us: body(): jnp.einsum('lmd,lmf->ldf', scaled_rows, saved_rows, preferred_element_typ...]
    unnamed x12 -> x4, local copies, waits for them, and re-layouts: 1.86 us -> 6.82 us
    broadcast_in_dim x1 -> x0, other arithmetic: 1.76 us -> none  [body(): hidden_grad = (own_prob[:, None] * summed).astype(jnp.bfloat16)[None]]
  transfers between devices with their start and end apart: 4 -> 0, of which waited for: 3 -> 0; matrix products, arithmetic and copies ran while one was open for 13% -> 0% of each run, Pallas kernels for 0% -> 0%
where the time goes in v1:
time: 84.7 us; the launch traced here: 83.5 us
  Pallas kernels  76 us (90%)
  local copies, waits for them, and re-layouts  6.82 us (8%)
    pallas_call x1, Pallas kernels, body(): pl.pallas_call(functools.partial(kernel, n), out_shape=(jax.ShapeDtypeStr...  76 us
    unnamed x4, local copies, waits for them, and re-layouts  6.82 us

profile of v1, /device:TPU:1, one launch (start us, length us, event | category | flops | bytes accessed | tf_op | source)
XLA Modules:
  0.0 83.5 jit_solution(14238206371083162975)
XLA Ops:
  0.6 1.4 %copy.9.ids_ref = s32[128,8]{1,0:T(8,128)} copy(s32[128,8]{0,1:T(8,128)} %param.7) | data formatting | bytes 8192 | tf_op args[1]
  2.0 76.0 %shard_map.85 = (bf16[2,256,1024]{2,1,0:T(8,128)(2,1)}, bf16[128,1024]{1,0:T(8,128)(2,1)}, bf16[128,256]{1,0:T(8,128)(2,1)}) custom-call(bf16[128,256]{1,0:T(8,128)(2,1)} %og_ref.1, s32[128,8]{1,0:T(8,128)} %copy.9.ids_ref, f32[128,128]{1,0:T(8,128)} %lg_ref.1, bf16[128,256]{1,0:T(8,128)(2,1)} %rw_ref.1, bf16[2,256,1024]{2,1,0:T(8,128)(2,1)} %ew_ref.1, ...), custom_call_target="tpu_custom_call" | custom-call | tf_op jit(solution)/shard_map/pallas_call | solution.py:414
  78.1 2.3 %copy.13 = bf16[2,256,1024]{2,1,0:T(8,128)(2,1)} copy(bf16[2,256,1024]{2,1,0:T(8,128)(2,1)} %get-tuple-element.12) | data formatting | bytes 2097152
  80.3 1.7 %copy.14 = bf16[1,128,1024]{2,1,0:T(8,128)(2,1)} copy(bf16[1,128,1024]{2,1,0:T(8,128)(2,1)} %bitcast.3) | data formatting | bytes 524288
  82.0 1.5 %copy.15 = bf16[128,256]{1,0:T(8,128)(2,1)} copy(bf16[128,256]{1,0:T(8,128)(2,1)} %get-tuple-element.14) | data formatting | bytes 131072

commit v2 on v1

v2 whole, which is shorter than its diff:
```python
import functools
import jax
import jax.numpy as jnp
from jax import lax
from jax.experimental import pallas as pl
from jax.experimental.pallas import tpu as pltpu
from jax.sharding import PartitionSpec as P

route_scale = 2.5
cap = 16
unset = 255.0
bf16 = jnp.bfloat16
f32 = jnp.float32
MESH = pl.DeviceIdType.MESH


def iota(shape, dim):
    return lax.broadcasted_iota(jnp.int32, shape, dim)


def kernel(n, og_ref, ids_ref, lg_ref, rw_ref, ew_ref, hs_ref, wg_ref, hg_ref, ig_ref,
           ids_v, lg_v, rw_v, hs_v, w_v, wp_v, tok, tk, tbs0, tbs1, tb0, tb1, sb0, sb1, r0, r1, e0, e1,
           dacc, ds, dr, g_v, pb, sr, s_v, sa, bs, sc, ct, q_s, q_c, q_y, q_r,
           acc, snd, rcv, code_v, prob_v,
           loc_sem, t_send, s1_send, s1_recv, s2_send, s2_recv, d_send, d_recv, x_send, x_recv,
           a_send, a_recv, b_send, b_recv, y_send, y_recv, r_send, r_recv):
    tokens, half = og_ref.shape[0], og_ref.shape[1] // 2
    topk = ids_ref.shape[0]
    experts = lg_ref.shape[1]
    width = hs_v.shape[1]
    ge = 2 * n
    hn = n // 2
    ch = n * cap
    rows = hn * cap
    parts = 2
    wide_part = width // parts
    g = lax.axis_index("grp")
    k = lax.axis_index("ep")
    x, z = g // n, lax.rem(g, n)
    y, c = k // 2, lax.rem(k, 2)
    wrap = lambda v: lax.rem(v + 2 * n, n)
    at_x = lambda v: (v * n + z, k)
    at_z = lambda v: (x * n + v, k)
    at_y = lambda v: (g, v * 2 + c)
    partner = (g, y * 2 + 1 - c)

    def rcopy(src, dst, ss, rs, dev):
        return pltpu.make_async_remote_copy(
            src_ref=src, dst_ref=dst, send_sem=ss, recv_sem=rs, device_id=dev, device_id_type=MESH)

    barrier = pltpu.get_barrier_semaphore()
    for d in range(1, n):
        for at, me in ((at_x, x), (at_z, z), (at_y, y)):
            pl.semaphore_signal(barrier, inc=1, device_id=at(wrap(me + d)), device_id_type=MESH)
    pl.semaphore_signal(barrier, inc=1, device_id=partner, device_id_type=MESH)

    def local(src, dst, i):
        copy = pltpu.make_async_copy(src, dst, loc_sem.at[i])
        copy.start()
        return copy

    ids_in = local(ids_ref, ids_v, 0)
    lg_in = local(lg_ref, lg_v, 1)
    tok_in = [local(og_ref.at[:, p * half:(p + 1) * half], tok.at[p], 2 + p) for p in range(2)]
    w_in = local(ew_ref, w_v, 4)
    hs_in = local(hs_ref, hs_v, 5)
    rw_in = local(rw_ref, rw_v, 6)

    for p in range(2):
        tok_in[p].wait()
    pl.semaphore_wait(barrier, 3 * (n - 1) + 1)

    order = [d if i == 0 else n - d for d in range(1, hn + 1) for i in range(2)][: n - 1]

    def tok0(v):
        return rcopy(tok.at[0], tk.at[0, x], t_send.at[0, v], s1_recv.at[0, x], at_x(v))

    def tok1(v):
        return rcopy(tok.at[1], tk.at[1, z], t_send.at[1, v], s1_recv.at[1, z], at_z(v))

    for d in order:
        tok0(wrap(x + d)).start()
        tok1(wrap(z + d)).start()
    tk[0, x] = tok[0]
    tk[1, z] = tok[1]

    ids_in.wait()
    row_t = iota((experts, tokens), 0)
    member = jnp.zeros((experts, tokens), f32)
    for i in range(topk):
        member += (ids_v[i:i + 1, :] == row_t).astype(f32)
    upper = (iota((tokens, tokens), 0) < iota((tokens, tokens), 1)).astype(f32).astype(bf16)
    rank = jnp.dot(member.astype(bf16), upper, preferred_element_type=f32)
    code = jnp.where(member > 0.0, rank, unset)
    code_v[...] = code
    code_t = code.astype(bf16)
    row_e, col_e = iota((experts, experts), 0), iota((experts, experts), 1)
    perm = (col_e == (row_e // 2 % n) * ge + (row_e // ge) * 2 + row_e % 2).astype(f32).astype(bf16)
    code_p = jnp.dot(perm, code_t, preferred_element_type=f32).astype(bf16)
    lg_in.wait()
    chosen = member * jax.nn.sigmoid(lg_v[...].T)
    prob = route_scale * chosen / jnp.sum(chosen, axis=0, keepdims=True)
    prob_v[...] = prob
    prob_t = prob.astype(bf16)
    for v in range(n):
        tbs0[v, 0:ge, :] = code_t[v * ge:(v + 1) * ge, :]
        tbs0[v, ge:2 * ge, :] = prob_t[v * ge:(v + 1) * ge, :]
        tbs1[v] = code_p[v * ge:(v + 1) * ge, :]
    tb0[x] = tbs0[x]
    tb1[z] = tbs1[z]

    def tab0(v):
        return rcopy(tbs0.at[v], tb0.at[x], s1_send.at[0, v], s1_recv.at[2, x], at_x(v))

    def tab1(v):
        return rcopy(tbs1.at[v], tb1.at[z], s1_send.at[1, v], s1_recv.at[3, z], at_z(v))

    for d in order:
        tab0(wrap(x + d)).start()
        tab1(wrap(z + d)).start()

    slot_r = iota((ge, cap, tokens), 1).astype(f32)
    dacc[...] = jnp.zeros_like(dacc)

    def fill(path, table):
        hot = (table.astype(f32)[:, None, :] == slot_r).astype(f32).astype(bf16)
        hot = hot.reshape(ge * cap, tokens)
        return hot

    def out0(v, us):
        return rcopy(sb0.at[v, us], r0.at[z, us // 2, lax.rem(us, 2)], s2_send.at[0, v], s2_recv.at[0, z], at_z(v))

    def out1(v, us):
        return rcopy(sb1.at[v, us], r1.at[x // 2, lax.rem(x, 2), us], s2_send.at[1, v], s2_recv.at[1, x], at_x(v))

    def spread0(us):
        hot = fill(0, tb0[us, 0:ge, :])
        got = jnp.dot(hot, tk[0, us], preferred_element_type=f32).astype(bf16)
        sb0[:, us] = got.reshape(n, 2, cap, half)
        for d in order:
            out0(wrap(z + d), us).start()
        r0[z, us // 2, lax.rem(us, 2)] = sb0[z, us]
        table = tb0[us, ge:2 * ge, :]
        wide = jnp.concatenate([table] * n, axis=0)
        wide = jnp.where(iota((experts, tokens), 0) // ge == us, wide.astype(f32), 0.0).astype(bf16)
        dacc[...] += lax.dot_general(hot, wide, (((1,), (1,)), ((), ())), preferred_element_type=f32)

    def spread1(us):
        hot = fill(1, tb1[us])
        got = jnp.dot(hot, tk[1, us], preferred_element_type=f32).astype(bf16)
        sb1[:, us] = got.reshape(n, 2, cap, half)
        for d in order:
            out1(wrap(x + d), us).start()
        r1[x // 2, lax.rem(x, 2), us] = sb1[x, us]

    spread0(x)
    spread1(z)

    def arrive(j, carry):
        odd = lax.rem(j, 2)
        off = (j + 1) // 2
        off = odd * off + (1 - odd) * (n - off)
        ux, uz = wrap(x + off), wrap(z + off)
        rcopy(tok.at[0], tk.at[0, ux], t_send.at[0, 0], s1_recv.at[0, ux], partner).wait_recv()
        rcopy(tbs0.at[0], tb0.at[ux], s1_send.at[0, 0], s1_recv.at[2, ux], partner).wait_recv()
        spread0(ux)
        rcopy(tok.at[1], tk.at[1, uz], t_send.at[1, 0], s1_recv.at[1, uz], partner).wait_recv()
        rcopy(tbs1.at[0], tb1.at[uz], s1_send.at[1, 0], s1_recv.at[3, uz], partner).wait_recv()
        spread1(uz)
        return carry

    lax.fori_loop(1, n, arrive, 0)

    ds[...] = dacc[...].astype(bf16).reshape(n, 2 * cap, experts)
    dr[z] = ds[z]

    def dout(v):
        return rcopy(ds.at[v], dr.at[z], d_send.at[v], d_recv.at[z], at_z(v))

    for d in order:
        dout(wrap(z + d)).start()

    w_in.wait()
    w_out = rcopy(w_v, wp_v, x_send.at[0], x_recv.at[0], partner)
    w_out.start()

    hs_in.wait()
    tile = ch * n // 4

    def gmul(i, carry):
        l = i // 4
        at = pl.multiple_of(i * tile, tile)
        g_v[pl.ds(at, tile), :] = lax.dot_general(
            hs_v[pl.ds(at, tile), :], w_v[l], (((1,), (1,)), ((), ())), preferred_element_type=f32)
        return carry

    lax.fori_loop(0, 8, gmul, 0)

    ex0 = rcopy(r0.at[:, :, 1 - c], e0, x_send.at[1], x_recv.at[1], partner)
    ex1 = rcopy(r1.at[:, 1 - c], e1, x_send.at[2], x_recv.at[2], partner)

    def give0(v):
        rcopy(r0.at[v, :, 1 - c], e0.at[v], x_send.at[1], x_recv.at[1], partner).start()

    give0(z)
    for d in order:
        vx = wrap(x + d)
        rcopy(sb1.at[0], r1.at[vx // 2, lax.rem(vx, 2)], s2_send.at[1, 0], s2_recv.at[1, vx], partner).wait_recv()
    ex1.start()
    for d in order:
        vz = wrap(z + d)
        rcopy(sb0.at[0], r0.at[vz], s2_send.at[0, 0], s2_recv.at[0, vz], partner).wait_recv()
        give0(vz)

    def scores():
        eye = iota((ch, ch), 0) == iota((ch, ch), 1)
        for l in range(2):
            for xb in range(n):
                q = l * n * ch + xb * ch
                a0 = r0[:, xb // 2, xb % 2, l].reshape(ch, half).astype(f32)
                a1 = r1[xb // 2, xb % 2, :, l].reshape(ch, half).astype(f32)
                s = a0 * g_v[q:q + ch, :half] + a1 * g_v[q:q + ch, half:]
                s = jnp.sum(s, axis=1, keepdims=True)
                s_v[l * n + xb:l * n + xb + 1, :] = jnp.sum(jnp.where(eye, s, 0.0), axis=0, keepdims=True)

    def partial(chunk, d, own, other):
        l, xh = chunk // hn, lax.rem(chunk, hn)
        zs = pl.ds(d * hn, hn)
        if own:
            mine = jnp.concatenate(
                [r0[zs, xh, c, l].reshape(rows, half), r1[xh, c, zs, l].reshape(rows, half)], axis=1)
        if other:
            their = jnp.concatenate(
                [e0[zs, xh, l].reshape(rows, half), e1[xh, zs, l].reshape(rows, half)], axis=1)
        step = width // 4
        for j in range(4):
            cols = slice(j * step, (j + 1) * step)
            total = jnp.dot(mine, w_v[l, :, cols], preferred_element_type=f32) if own else acc[d, :, cols]
            if other:
                total = total + jnp.dot(their, wp_v[l, :, cols], preferred_element_type=f32)
            acc[d, :, cols] = total

    def hop(s, d, i, j):
        to = at_y(wrap(y + 1)) if d == 0 else at_y(wrap(y - 1 + n))
        return rcopy(snd.at[d, s, i, j], rcv.at[d, s, i, j], r_send.at[d, s, i, j], r_recv.at[d, s, i, j], to)

    def at_step(s, d):
        return wrap(y - 1 - s + n) if d == 0 else wrap(y + 1 + s)

    def ring(s):
        if s == 0:
            for d in range(2):
                partial(at_step(0, d), d, True, False)
            score_a()
            w_out.wait_recv()
            ex1.wait_recv()
            ex0.wait_recv()
            for d in range(2):
                partial(at_step(0, d), d, False, True)
        else:
            for d in range(2):
                partial(at_step(s, d), d, True, True)
        for i in range(hn):
            for j in range(parts):
                for d in range(2):
                    val = acc[d, i * cap:(i + 1) * cap, j * wide_part:(j + 1) * wide_part]
                    if s > 0:
                        hop(s - 1, d, i, j).wait_recv()
                        val = val + rcv[d, s - 1, i, j].astype(f32)
                    snd[d, s, i, j] = val.astype(bf16)
                    hop(s, d, i, j).start()

    def aout(v):
        return rcopy(s_v, sa.at[z], a_send.at[v], a_recv.at[z], at_z(v))

    def bout(v):
        return rcopy(bs.at[v], sc.at[x], b_send.at[v], b_recv.at[x], at_x(v))

    def yout(v):
        return rcopy(q_y, q_r.at[y], y_send.at[v], y_recv.at[y], at_y(v))

    qx = rcopy(q_s, q_c, x_send.at[3], x_recv.at[3], partner)

    def score_a():
        scores()
        sa[z] = s_v[...]
        for d in order:
            aout(wrap(z + d)).start()

    def score_b():
        for d in order:
            v = wrap(z + d)
            rcopy(s_v, sa.at[v], a_send.at[0], a_recv.at[v], partner).wait_recv()
        for v in range(n):
            for l in range(2):
                for xb in range(n):
                    bs[xb, v * 2 + l:v * 2 + l + 1, :] = sa[v, l * n + xb:l * n + xb + 1, :]
        sc[x] = bs[x]
        for d in order:
            bout(wrap(x + d)).start()

    def score_c():
        for d in order:
            v = wrap(x + d)
            rcopy(bs.at[0], sc.at[v], b_send.at[0], b_recv.at[v], partner).wait_recv()
        ct[...] = sc[...].reshape(experts, ch).T
        q_s[...] = ct[pl.ds(pl.multiple_of(z * cap, cap), cap), :]
        qx.start()

    def score_d():
        qx.wait_recv()
        q_y[...] = q_s[...] + q_c[...]
        q_r[y] = q_y[...]
        for d in order:
            yout(wrap(y + d)).start()

    def finish():
        rw_in.wait()
        for d in order:
            v = wrap(y + d)
            rcopy(q_y, q_r.at[v], y_send.at[0], y_recv.at[v], partner).wait_recv()
        total = q_r[0]
        for v in range(1, n):
            total = total + q_r[v]
        codes = code_v[...].T
        pair = jnp.zeros((tokens, experts), f32)
        for r in range(cap):
            pair += jnp.where(codes == float(r), total[r:r + 1, :], 0.0)
        probs = prob_v[...].T
        mean = jnp.sum(probs * pair, axis=1, keepdims=True) / route_scale
        grad = (probs * (1.0 - jax.nn.sigmoid(lg_v[...])) * (pair - mean)).astype(bf16)
        ig_ref[...] = jnp.dot(grad, rw_v[...], preferred_element_type=f32).astype(bf16)

    def probs_in():
        for d in order:
            v = wrap(z + d)
            rcopy(ds.at[0], dr.at[v], d_send.at[0], d_recv.at[v], partner).wait_recv()
        mine = dr[...].reshape(n * 2 * cap, experts).astype(f32)
        shape = (n * 2 * cap, experts)
        keep = iota(shape, 1) % ge == z * 2 + iota(shape, 0) // cap % 2
        mine = jnp.where(keep, mine, 0.0).astype(bf16)
        wide = (experts, n * half)
        pick = (iota(wide, 0) // ge == iota(wide, 1) // half).astype(f32).astype(bf16)
        pb[...] = jnp.dot(mine, pick, preferred_element_type=f32).reshape(n, 2, cap, n * half)

    def scale(l):
        for xb in range(n):
            p = pb[:, l, :, xb * half:(xb + 1) * half].reshape(ch, half)
            a0 = r0[:, xb // 2, xb % 2, l].reshape(ch, half).astype(f32)
            a1 = r1[xb // 2, xb % 2, :, l].reshape(ch, half).astype(f32)
            sr[l, xb * ch:(xb + 1) * ch, :half] = (p * a0).astype(bf16)
            sr[l, xb * ch:(xb + 1) * ch, half:] = (p * a1).astype(bf16)

    def grads(i):
        l, j = i // 4, i % 4
        step = width // 4
        cols = slice(j * step, (j + 1) * step)
        wg_ref[l, :, cols] = lax.dot_general(
            sr[l], hs_v[l * n * ch:(l + 1) * n * ch, cols], (((0,), (0,)), ((), ())),
            preferred_element_type=f32).astype(bf16)

    some = lambda f, *items: [functools.partial(f, i) for i in items]
    todo = [[probs_in], [score_b] + some(scale, 0), some(grads, 0, 1), [score_c] + some(scale, 1),
            [score_d] + some(grads, 2, 3), some(grads, 4, 5), some(grads, 6, 7) + [finish]]
    if n < 8:
        todo = [sum(todo, [])]
    for s in range(n - 1):
        ring(s)
        for work in todo[s]:
            work()
    for d in range(2):
        partial(y, d, True, True)
    mine_l, mine_x = k // n, lax.rem(k, n)
    for i in range(hn):
        for j in range(parts):
            for d in range(2):
                hop(n - 2, d, i, j).wait_recv()
                zb = d * hn + i
                p = pb[zb, mine_l, :, pl.ds(pl.multiple_of(mine_x * half, half), half)]
                for m in range(wide_part // half):
                    a, b = j * wide_part + m * half, j * wide_part + (m + 1) * half
                    val = acc[d, i * cap:(i + 1) * cap, a:b]
                    val = val + rcv[d, n - 2, i, j, :, m * half:(m + 1) * half].astype(f32)
                    hg_ref[zb * cap:(zb + 1) * cap, a:b] = (p * val).astype(bf16)

    w_out.wait_send()
    ex0.wait_send()
    ex1.wait_send()
    qx.wait_send()
    for d in order:
        vx, vz, vy = wrap(x + d), wrap(z + d), wrap(y + d)
        tok0(vx).wait_send()
        tok1(vz).wait_send()
        tab0(vx).wait_send()
        tab1(vz).wait_send()
        rcopy(sb0.at[vz], r0.at[z], s2_send.at[0, vz], s2_recv.at[0, z], partner).wait_send()
        rcopy(sb1.at[vx], r1.at[x // 2, lax.rem(x, 2)], s2_send.at[1, vx], s2_recv.at[1, x], partner).wait_send()
        dout(vz).wait_send()
        aout(vz).wait_send()
        bout(vx).wait_send()
        yout(vy).wait_send()
    for s in range(n - 1):
        for i in range(hn):
            for j in range(parts):
                for d in range(2):
                    hop(s, d, i, j).wait_send()


def put_out(wg_ref, hg_ref, ig_ref, wg_out, hg_out, ig_out, sem):
    copies = [
        pltpu.make_async_copy(src, dst, sem.at[i])
        for i, (src, dst) in enumerate(((wg_ref, wg_out), (hg_ref, hg_out), (ig_ref, ig_out)))
    ]
    for copy in copies:
        copy.start()
    for copy in copies:
        copy.wait()


def body(n, out_grad, expert_ids, router_logits, router_weight, expert_weight, hidden_saved):
    tokens, features = out_grad.shape
    half = features // 2
    experts = router_logits.shape[1]
    width = expert_weight.shape[2]
    slots = hidden_saved.shape[1]
    ge, hn, ch = 2 * n, n // 2, n * cap
    rows, parts = hn * cap, 2
    vm = pltpu.VMEM
    dma = pltpu.SemaphoreType.DMA
    scratch = [
        vm(expert_ids.shape[::-1], jnp.int32), vm((tokens, experts), f32), vm((experts, features), bf16),
        vm((slots, width), bf16), vm((2, features, width), bf16), vm((2, features, width), bf16),
        vm((2, tokens, half), bf16), vm((2, n, tokens, half), bf16),
        vm((n, 2 * ge, tokens), bf16), vm((n, ge, tokens), bf16),
        vm((n, 2 * ge, tokens), bf16), vm((n, ge, tokens), bf16),
        vm((n, n, 2, cap, half), bf16), vm((n, n, 2, cap, half), bf16),
        vm((n, hn, 2, 2, cap, half), bf16), vm((hn, 2, n, 2, cap, half), bf16),
        vm((n, hn, 2, cap, half), bf16), vm((hn, n, 2, cap, half), bf16),
        vm((ge * cap, experts), f32), vm((n, 2 * cap, experts), bf16), vm((n, 2 * cap, experts), bf16),
        vm((slots, features), f32), vm((n, 2, cap, n * half), f32), vm((2, n * ch, features), bf16),
        vm((ge, ch), f32), vm((n, ge, ch), f32), vm((n, ge, ch), f32), vm((n, ge, ch), f32),
        vm((ch, experts), f32),
        vm((cap, experts), f32), vm((cap, experts), f32), vm((cap, experts), f32), vm((n, cap, experts), f32),
        vm((2, rows, width), f32), vm((2, n - 1, hn, parts, cap, width // parts), bf16),
        vm((2, n - 1, hn, parts, cap, width // parts), bf16),
        vm((experts, tokens), f32), vm((experts, tokens), f32),
        dma((7,)), dma((2, n)), dma((2, n)), dma((4, n)), dma((2, n)), dma((2, n)), dma((n,)), dma((n,)),
        dma((4,)), dma((4,)), dma((n,)), dma((n,)), dma((n,)), dma((n,)), dma((n,)), dma((n,)),
        dma((2, n - 1, hn, parts)), dma((2, n - 1, hn, parts)),
    ]
    in_vmem = pl.BlockSpec(memory_space=pltpu.VMEM)
    in_hbm = pl.BlockSpec(memory_space=pltpu.HBM)
    weight_grad, hidden_grad, input_grad = pl.pallas_call(
        functools.partial(kernel, n),
        out_shape=(
            pltpu.VMEM((2, features, width), bf16),
            pltpu.VMEM((ch, width), bf16),
            pltpu.VMEM((tokens, features), bf16),
        ),
        in_specs=[in_hbm] * 6,
        out_specs=(in_vmem, in_vmem, in_vmem),
        scratch_shapes=scratch,
        compiler_params=pltpu.CompilerParams(collective_id=0, has_side_effects=True),
    )(out_grad, expert_ids.T, router_logits, router_weight, expert_weight, hidden_saved.reshape(slots, width))
    weight_grad, hidden_grad, input_grad = pl.pallas_call(
        put_out,
        out_shape=(
            jax.ShapeDtypeStruct((2, features, width), bf16),
            jax.ShapeDtypeStruct((ch, width), bf16),
            jax.ShapeDtypeStruct((tokens, features), bf16),
        ),
        in_specs=[pl.BlockSpec(memory_space=pl.ANY)] * 3,
        out_specs=(in_hbm, in_hbm, in_hbm),
        scratch_shapes=[dma((3,))],
        compiler_params=pltpu.CompilerParams(vmem_limit_bytes=1 << 20),
    )(weight_grad, hidden_grad, input_grad)
    return weight_grad, hidden_grad[None], input_grad


def solution(mesh):
    n = mesh.shape["ep"] // 2
    in_specs = (
        P("grp", "ep"),
        P("grp", None),
        P("grp", None),
        P(None, "ep"),
        P("grp", "ep", None),
        P("grp", None, None),
    )
    out_specs = (P("grp", "ep", None), P("grp", "ep", None), P("grp", "ep"))
    return jax.shard_map(functools.partial(body, n), mesh=mesh, in_specs=in_specs, out_specs=out_specs, check_vma=False)
```

time: 84.7 us -> 75.2 us (0.89); the launches traced: 83.5 us -> 75.1 us
  local copies, waits for them, and re-layouts: 6.82 us -> 0 us
  Pallas kernels: 76 us -> 74.5 us
    unnamed x4 -> x0, local copies, waits for them, and re-layouts: 6.82 us -> none
    pallas_call x1 -> x2, Pallas kernels: 76 us -> 74.5 us  [the longest x1 73.4 us: body(): pl.pallas_call(functools.partial(kernel, n), out_shape=(pltpu.VMEM((2, fe...]
where the time goes in v2:
time: 75.2 us; the launch traced here: 75.1 us
  Pallas kernels  74.5 us (99%)
    pallas_call x1, Pallas kernels, body(): pl.pallas_call(functools.partial(kernel, n), out_shape=(pltpu.VMEM((2, fe...  73.4 us

profile of v2, /device:TPU:1, one launch (start us, length us, event | category | flops | bytes accessed | tf_op | source)
XLA Modules:
  0.0 75.1 jit_solution(18279142671476604637)
XLA Ops:
  0.6 73.4 %shard_map.85 = (bf16[2,256,1024]{2,1,0:T(8,128)(2,1)S(1)}, bf16[128,1024]{1,0:T(8,128)(2,1)S(1)}, bf16[128,256]{1,0:T(8,128)(2,1)S(1)}) custom-call(bf16[128,256]{1,0:T(8,128)(2,1)} %og_ref.1, s32[8,128]{1,0:T(8,128)} %bitcast.4, f32[128,128]{1,0:T(8,128)} %lg_ref.1, bf16[128,256]{1,0:T(8,128)(2,1)} %rw_ref.1, bf16[2,256,1024]{2,1,0:T(8,128)(2,1)} %ew_ref.1, ...), custom_call_target="tpu_custom_call" | custom-call | tf_op jit(solution)/shard_map/pallas_call | solution.py:453
  74.0 1.1 %shard_map.86 = (bf16[2,256,1024]{2,1,0:T(8,128)(2,1)}, bf16[128,1024]{1,0:T(8,128)(2,1)}, bf16[128,256]{1,0:T(8,128)(2,1)}) custom-call(bf16[2,256,1024]{2,1,0:T(8,128)(2,1)S(1)} %get-tuple-element.9.wg_ref, bf16[128,1024]{1,0:T(8,128)(2,1)S(1)} %get-tuple-element.10.hg_ref, bf16[128,256]{1,0:T(8,128)(2,1)S(1)} %get-tuple-element.11.ig_ref), custom_call_target="tpu_custom_call" | custom-call | tf_op jit(solution)/shard_map/pallas_call | solution.py:465

commit v3 on v2

--- a/solution.py
+++ b/solution.py
@@ -78,7 +78,8 @@
     def tok1(v):
         return rcopy(tok.at[1], tk.at[1, z], t_send.at[1, v], s1_recv.at[1, z], at_z(v))
 
-    for d in order:
+    near = order[:4]
+    for d in near:
         tok0(wrap(x + d)).start()
         tok1(wrap(z + d)).start()
     tk[0, x] = tok[0]
@@ -109,6 +110,20 @@
     tb0[x] = tbs0[x]
     tb1[z] = tbs1[z]
 
+    relays = [(2, -1, 3), (2, -2, 4), (n - 2, 1, 5)] if n > 4 else []
+
+    def far0(off, d, i):
+        u = wrap(x + off)
+        return rcopy(tk.at[0, u], tk.at[0, u], t_send.at[0, wrap(x + i)], s1_recv.at[0, u], at_x(wrap(x + d)))
+
+    def far1(off, d, i):
+        u = wrap(z + off)
+        return rcopy(tk.at[1, u], tk.at[1, u], t_send.at[1, wrap(z + i)], s1_recv.at[1, u], at_z(wrap(z + d)))
+
+    def rows_in(ux, uz):
+        rcopy(tok.at[0], tk.at[0, ux], t_send.at[0, 0], s1_recv.at[0, ux], partner).wait_recv()
+        rcopy(tok.at[1], tk.at[1, uz], t_send.at[1, 0], s1_recv.at[1, uz], partner).wait_recv()
+
     def tab0(v):
         return rcopy(tbs0.at[v], tb0.at[x], s1_send.at[0, v], s1_recv.at[2, x], at_x(v))
 
@@ -155,16 +170,24 @@
 
     spread0(x)
     spread1(z)
+    if relays:
+        for off in (2, n - 2):
+            rows_in(wrap(x + off), wrap(z + off))
+        for relay in relays:
+            far0(*relay).start()
+            far1(*relay).start()
 
     def arrive(j, carry):
         odd = lax.rem(j, 2)
         off = (j + 1) // 2
         off = odd * off + (1 - odd) * (n - off)
         ux, uz = wrap(x + off), wrap(z + off)
-        rcopy(tok.at[0], tk.at[0, ux], t_send.at[0, 0], s1_recv.at[0, ux], partner).wait_recv()
+        if relays:
+            pl.when((j - 3) * (j - 4) > 0)(lambda: rows_in(ux, uz))
+        else:
+            rows_in(ux, uz)
         rcopy(tbs0.at[0], tb0.at[ux], s1_send.at[0, 0], s1_recv.at[2, ux], partner).wait_recv()
         spread0(ux)
-        rcopy(tok.at[1], tk.at[1, uz], t_send.at[1, 0], s1_recv.at[1, uz], partner).wait_recv()
         rcopy(tbs1.at[0], tb1.at[uz], s1_send.at[1, 0], s1_recv.at[3, uz], partner).wait_recv()
         spread1(uz)
         return carry
@@ -389,8 +412,6 @@
     qx.wait_send()
     for d in order:
         vx, vz, vy = wrap(x + d), wrap(z + d), wrap(y + d)
-        tok0(vx).wait_send()
-        tok1(vz).wait_send()
         tab0(vx).wait_send()
         tab1(vz).wait_send()
         rcopy(sb0.at[vz], r0.at[z], s2_send.at[0, vz], s2_recv.at[0, z], partner).wait_send()
@@ -399,6 +420,12 @@
         aout(vz).wait_send()
         bout(vx).wait_send()
         yout(vy).wait_send()
+    for d in near:
+        tok0(wrap(x + d)).wait_send()
+        tok1(wrap(z + d)).wait_send()
+    for relay in relays:
+        far0(*relay).wait_send()
+        far1(*relay).wait_send()
     for s in range(n - 1):
         for i in range(hn):
             for j in range(parts):

time: 75.2 us -> 73.9 us (0.983)
  Pallas kernels: 74.5 us -> 72.7 us
    pallas_call x1, Pallas kernels: 73.4 us -> 71.6 us  [body(): pl.pallas_call(functools.partial(kernel, n), out_shape=(pltpu.VMEM((2, fe...]
where the time goes in v3:
time: 73.9 us; the launch traced here: 73.3 us
  Pallas kernels  72.7 us (98%)
    pallas_call x1, Pallas kernels, body(): pl.pallas_call(functools.partial(kernel, n), out_shape=(pltpu.VMEM((2, fe...  71.6 us

profile of v3, /device:TPU:1, one launch (start us, length us, event | category | flops | bytes accessed | tf_op | source)
XLA Modules:
  0.0 73.3 jit_solution(18186639193961974436)
XLA Ops:
  0.6 71.6 %shard_map.85 = (bf16[2,256,1024]{2,1,0:T(8,128)(2,1)S(1)}, bf16[128,1024]{1,0:T(8,128)(2,1)S(1)}, bf16[128,256]{1,0:T(8,128)(2,1)S(1)}) custom-call(bf16[128,256]{1,0:T(8,128)(2,1)} %og_ref.1, s32[8,128]{1,0:T(8,128)} %bitcast.4, f32[128,128]{1,0:T(8,128)} %lg_ref.1, bf16[128,256]{1,0:T(8,128)(2,1)} %rw_ref.1, bf16[2,256,1024]{2,1,0:T(8,128)(2,1)} %ew_ref.1, ...), custom_call_target="tpu_custom_call" | custom-call | tf_op jit(solution)/shard_map/pallas_call | solution.py:480
  72.2 1.1 %shard_map.86 = (bf16[2,256,1024]{2,1,0:T(8,128)(2,1)}, bf16[128,1024]{1,0:T(8,128)(2,1)}, bf16[128,256]{1,0:T(8,128)(2,1)}) custom-call(bf16[2,256,1024]{2,1,0:T(8,128)(2,1)S(1)} %get-tuple-element.9.wg_ref, bf16[128,1024]{1,0:T(8,128)(2,1)S(1)} %get-tuple-element.10.hg_ref, bf16[128,256]{1,0:T(8,128)(2,1)S(1)} %get-tuple-element.11.ig_ref), custom_call_target="tpu_custom_call" | custom-call | tf_op jit(solution)/shard_map/pallas_call | solution.py:492

commit v4 on v3

--- a/solution.py
+++ b/solution.py
@@ -280,6 +280,12 @@
             ex0.wait_recv()
             for d in range(2):
                 partial(at_step(0, d), d, False, True)
+                for i in range(hn):
+                    for j in range(parts):
+                        val = acc[d, i * cap:(i + 1) * cap, j * wide_part:(j + 1) * wide_part]
+                        snd[d, 0, i, j] = val.astype(bf16)
+                        hop(0, d, i, j).start()
+            return
         else:
             for d in range(2):
                 partial(at_step(s, d), d, True, True)
@@ -287,9 +293,8 @@
             for j in range(parts):
                 for d in range(2):
                     val = acc[d, i * cap:(i + 1) * cap, j * wide_part:(j + 1) * wide_part]
-                    if s > 0:
-                        hop(s - 1, d, i, j).wait_recv()
-                        val = val + rcv[d, s - 1, i, j].astype(f32)
+                    hop(s - 1, d, i, j).wait_recv()
+                    val = val + rcv[d, s - 1, i, j].astype(f32)
                     snd[d, s, i, j] = val.astype(bf16)
                     hop(s, d, i, j).start()
 

time: 73.9 us -> 73.9 us (level)
  no operation moved by 1% of the time
where the time goes in v4:
time: 73.9 us; the launch traced here: 73.5 us
  Pallas kernels  72.8 us (99%)
    pallas_call x1, Pallas kernels, body(): pl.pallas_call(functools.partial(kernel, n), out_shape=(pltpu.VMEM((2, fe...  71.7 us

profile of v4, /device:TPU:1, one launch (start us, length us, event | category | flops | bytes accessed | tf_op | source)
XLA Modules:
  0.0 73.5 jit_solution(8427189485735007350)
XLA Ops:
  0.6 71.7 %shard_map.85 = (bf16[2,256,1024]{2,1,0:T(8,128)(2,1)S(1)}, bf16[128,1024]{1,0:T(8,128)(2,1)S(1)}, bf16[128,256]{1,0:T(8,128)(2,1)S(1)}) custom-call(bf16[128,256]{1,0:T(8,128)(2,1)} %og_ref.1, s32[8,128]{1,0:T(8,128)} %bitcast.4, f32[128,128]{1,0:T(8,128)} %lg_ref.1, bf16[128,256]{1,0:T(8,128)(2,1)} %rw_ref.1, bf16[2,256,1024]{2,1,0:T(8,128)(2,1)} %ew_ref.1, ...), custom_call_target="tpu_custom_call" | custom-call | tf_op jit(solution)/shard_map/pallas_call | solution.py:485
  72.4 1.1 %shard_map.86 = (bf16[2,256,1024]{2,1,0:T(8,128)(2,1)}, bf16[128,1024]{1,0:T(8,128)(2,1)}, bf16[128,256]{1,0:T(8,128)(2,1)}) custom-call(bf16[2,256,1024]{2,1,0:T(8,128)(2,1)S(1)} %get-tuple-element.9.wg_ref, bf16[128,1024]{1,0:T(8,128)(2,1)S(1)} %get-tuple-element.10.hg_ref, bf16[128,256]{1,0:T(8,128)(2,1)S(1)} %get-tuple-element.11.ig_ref), custom_call_target="tpu_custom_call" | custom-call | tf_op jit(solution)/shard_map/pallas_call | solution.py:497
